TPU v7x, 512 devices: a whole 4x8x8 slice. The times are simulated.
512 devices in a mesh: expert: 128 (over x, z, y_lo), hidden: 4 (over y_hi, core).
Axes of the slice: x: 4, y: 8 (y_hi: 2, y_lo: 4; y = y_hi * 4 + y_lo), z: 8, core: 2. Of those that a mesh axis runs over, the one named last changes fastest.
Arguments:
- tokens: bfloat16 [512, 196, 1024], P(('expert', 'hidden')), may hold values from -40 to 40
- router: bfloat16 [1024, 128], replicated, may hold values from -0.5 to 0.5
- w_in: bfloat16 [128, 1024, 3072], P('expert', None, 'hidden'), may hold values from -0.1875 to 0.1875
- b_in: float32 [128, 3072], P('expert', 'hidden'), may hold values from -6 to 6
- w_out: bfloat16 [128, 3072, 1024], P('expert', 'hidden'), may hold values from -0.109375 to 0.109375
- cotangent: bfloat16 [512, 196, 1024], P(('expert', 'hidden')), may hold values from -6 to 6
Outputs:
- mixed: bfloat16 [512, 196, 1024], P(('expert', 'hidden'))
- token_grad: bfloat16 [512, 196, 1024], P(('expert', 'hidden'))
All inputs are finite; a program needn't handle non-finite values.
Results may differ from a plain program's by a relative error of at most 0.015.
Values may be sent and summed in bfloat16 or wider, within the bound.
No kernel may reach another device: no remote copies, remote signals or barrier semaphores. Data moves between devices by JAX's collectives and lax.ppermute only.
A program may use at most 64 MiB of HBM per device.

v0:
```python
import jax
import jax.numpy as jnp
from jax import lax
from jax.sharding import PartitionSpec as P


def split_up(x, dim, devices):
    shape = x.shape
    parts = x.reshape(*shape[:dim], devices, shape[dim] // devices, *shape[dim + 1 :])
    return jnp.moveaxis(parts, dim, 0)


def sum_at_owner(x, axis, dim):
    devices = lax.axis_size(axis)
    parts = lax.all_to_all(split_up(x, dim, devices), axis, 0, 0, tiled=True)
    return jnp.sum(parts.astype(jnp.float32), axis=0)


def outbound(stacked):
    moved = lax.all_to_all(stacked, "expert", split_axis=2, concat_axis=1, tiled=True)
    return lax.all_gather(moved, "hidden", axis=1, tiled=True)


def inbound(terms):
    summed = sum_at_owner(terms.astype(jnp.bfloat16), "hidden", 1)
    return lax.all_to_all(
        summed.astype(jnp.bfloat16), "expert", split_axis=1, concat_axis=2, tiled=True
    )


def expert_forward(slots, w_in, b_in, w_out):
    pre = jnp.einsum("red,edf->ref", slots, w_in, preferred_element_type=jnp.float32) + b_in[None]
    act = jax.nn.gelu(pre).astype(jnp.bfloat16)
    return (jnp.einsum("ref,efd->red", act, w_out, preferred_element_type=jnp.float32), pre)


def expert_backward(grads, pre, w_in, w_out):
    act_grad = jnp.einsum("red,efd->ref", grads, w_out, preferred_element_type=jnp.float32)
    _, pull = jax.vjp(jax.nn.gelu, pre)
    pre_grad = pull(act_grad)[0].astype(jnp.bfloat16)
    return jnp.einsum("ref,edf->red", pre_grad, w_in, preferred_element_type=jnp.float32)


def shards(tokens, router, w_in, b_in, w_out, cotangent):
    logits = jnp.einsum("bmd,ds->bms", tokens, router, preferred_element_type=jnp.float32)
    dispatch = jax.nn.softmax(logits, axis=1)
    combine = jax.nn.softmax(logits, axis=2)
    dispatch_w = dispatch.astype(jnp.bfloat16)
    combine_w = combine.astype(jnp.bfloat16)
    slot_in = jnp.einsum(
        "bms,bmd->bsd", dispatch_w, tokens, preferred_element_type=jnp.float32
    ).astype(jnp.bfloat16)
    slot_cot = jnp.einsum(
        "bms,bmd->bsd", combine_w, cotangent, preferred_element_type=jnp.float32
    ).astype(jnp.bfloat16)
    arrived = outbound(jnp.stack([slot_in, slot_cot]))
    partial_value, pre = expert_forward(arrived[0], w_in, b_in, w_out)
    gpartial = expert_backward(arrived[1], pre, w_in, w_out)
    returned = inbound(jnp.stack([partial_value, gpartial]))
    slot_out = returned[0]
    slot_grad = returned[1]
    mixed = jnp.einsum(
        "bms,bsd->bmd", combine_w, slot_out, preferred_element_type=jnp.float32
    ).astype(jnp.bfloat16)
    combine_grad = jnp.einsum(
        "bmd,bsd->bms", cotangent, slot_out, preferred_element_type=jnp.float32
    )
    dispatch_grad = jnp.einsum(
        "bmd,bsd->bms", tokens, slot_grad, preferred_element_type=jnp.float32
    )
    logit_grad = combine * (combine_grad - jnp.sum(combine * combine_grad, axis=2, keepdims=True))
    logit_grad = logit_grad + dispatch * (
        dispatch_grad - jnp.sum(dispatch * dispatch_grad, axis=1, keepdims=True)
    )
    logit_grad = logit_grad.astype(jnp.bfloat16)
    token_grad = jnp.einsum(
        "bms,bsd->bmd", dispatch_w, slot_grad, preferred_element_type=jnp.float32
    )
    token_grad = token_grad + jnp.einsum(
        "bms,ds->bmd", logit_grad, router, preferred_element_type=jnp.float32
    )
    return (mixed, token_grad.astype(jnp.bfloat16))


def solution(mesh):
    return jax.shard_map(
        shards,
        mesh=mesh,
        in_specs=(
            P(("expert", "hidden"), None, None),
            P(),
            P("expert", None, "hidden"),
            P("expert", "hidden"),
            P("expert", "hidden", None),
            P(("expert", "hidden"), None, None),
        ),
        out_specs=(P(("expert", "hidden"), None, None), P(("expert", "hidden"), None, None)),
        check_vma=False,
    )
```

profile of v0, /device:TPU:1, one launch (start us, length us, event | category | flops | bytes accessed | tf_op | source)
XLA Modules:
  0.0 200.0 jit_solution(14822342059811094486)
XLA Ops:
  7.2 0.0 copy-start
  7.2 0.0 copy-start.3
  7.2 0.0 all-gather.3.cloned.1.call-start
  7.2 1.6 fusion.82
  8.8 0.2 fusion.59
  9.0 1.3 fusion.35
  10.3 0.0 copy-done.3
  10.3 0.4 fusion.36
  10.7 0.1 pad_maximum_fusion
  10.7 0.5 copy.17
  11.3 0.0 copy-start.4
  11.3 37.1 %all_to_all.26 = bf16[2,1,128,1024]{3,0,1,2:T(2,128)(2,1)S(1)} all-to-all(bf16[2,1,128,1024]{3,0,1,2:T(2,128)(2,1)S(1)} %copy.17), channel_id=1, replica_groups=mesh['expert'=128,'hidden'=4] {'expert'}, dimensions={2} | all-to-all | bytes 1048576 | tf_op jit(solution)/shard_map/all_to_all | solution.py:20
  48.4 0.9 copy.18
  49.3 0.0 all-gather.3.cloned.1.call-update
  49.3 0.0 copy-done.4
  49.4 39.7 %all-gather.3.cloned.1.call-done = bf16[2,1,512,1024]{3,2,1,0:T(8,128)(2,1)} async-done(((bf16[2,1,128,1024]{3,2,1,0:T(8,128)(2,1)}), bf16[2,1,512,1024]{3,2,1,0:T(8,128)(2,1)}) %all-gather.3.cloned.1.call-update) | async-done | bytes 2097168 | tf_op jit(solution)/shard_map/all_gather | solution.py:21
  89.1 2.7 %fusion.7 = f32[512,1,768]{2,0,1:T(8,128)S(1)} fusion(bf16[1,1024,768]{2,1,0:T(8,128)(2,1)} %param.8, bf16[2,1,512,1024]{3,2,1,0:T(8,128)(2,1)} %all-gather.3.cloned.1.call-done, f32[768]{0:T(1024)S(1)} %reduce.14), kind=kOutput, calls=%fused_computation.11 | convolution fusion | flops 805699584 | bytes 4197376 | tf_op jit(solution)/shard_map/red,edf->ref/dot_general | solution.py:32
  91.8 0.0 copy-start.5
  91.8 1.1 copy-done.5
  92.9 0.0 copy-done
  92.9 1.1 fusion.22
  94.1 6.1 %fusion.19 = bf16[512,1024]{1,0:T(8,128)(2,1)} fusion(bf16[1,1024,768]{2,1,0:T(8,128)(2,1)} %param.8, f32[512,1,768]{2,0,1:T(8,128)} %copy-done.5, bf16[1,768,1024]{2,1,0:T(8,128)(2,1)S(1)} %copy-done, bf16[2,1,512,1024]{3,2,1,0:T(8,128)(2,1)} %all-gather.3.cloned.1.call-done), kind=kOutput, calls=%fused_computation.26 | convolution fusion | flops 1619001344 | bytes 6815744 | tf_op jit(solution)/shard_map/ref,edf->red/dot_general | solution.py:41
  100.1 1.4 maximum_bitcast_fusion
  101.5 45.0 %all_to_all.27 = bf16[4,2,128,1,1024]{4,2,3,1,0:T(8,128)(2,1)} all-to-all(bf16[4,2,128,1,1024]{4,2,3,1,0:T(8,128)(2,1)S(1)} %maximum_bitcast_fusion), channel_id=1, replica_groups=mesh['expert'=128,'hidden'=4] {'hidden'}, dimensions={0} | all-to-all | bytes 4194304 | tf_op jit(solution)/shard_map/all_to_all | solution.py:15
  146.6 2.0 %reduce_sum.52 = bf16[2,128,1024]{2,1,0:T(8,128)(2,1)S(1)} reduce(bf16[4,2,128,1,1024]{4,2,3,1,0:T(8,128)(2,1)} %all_to_all.27, bf16[]{:T(256)} %constant.19.clone.1), dimensions={0,3}, to_apply=%region_4.0 | reduce | flops 786432 | bytes 2621442 | tf_op jit(solution)/shard_map/reduce_sum | solution.py:16
  148.6 0.5 copy.21
  149.1 0.0 copy-start.1
  149.2 40.0 %all_to_all.28 = bf16[2,128,1,1024]{3,0,2,1:T(2,128)(2,1)S(1)} all-to-all(bf16[2,128,1,1024]{3,0,2,1:T(2,128)(2,1)S(1)} %copy.21), channel_id=1, replica_groups=mesh['expert'=128,'hidden'=4] {'expert'}, dimensions={1} | all-to-all | bytes 1048576 | tf_op jit(solution)/shard_map/all_to_all | solution.py:26
  189.2 0.7 fusion.83
  189.9 0.0 copy-done.1
  189.9 0.3 convolution_bitcast_fusion
  190.2 0.0 copy-start.2
  190.2 0.3 fusion.55
  190.5 1.1 fusion.34
  191.6 0.4 multiply_reduce_fusion.1
  192.0 0.0 copy-done.2
  192.0 1.1 fusion.33
  (1 shorter events, 0.0 us)
Async XLA Ops:
  7.2 85.8 %copy-start = (bf16[1,768,1024]{2,1,0:T(8,128)(2,1)S(1)}, bf16[1,768,1024]{2,1,0:T(8,128)(2,1)}, u32[]{:S(2)}) copy-start(bf16[1,768,1024]{2,1,0:T(8,128)(2,1)} %param.10) | copy-start | bytes 4718596
  7.2 3.1 %copy-start.3 = (bf16[1,196,1024]{2,1,0:T(8,128)(2,1)S(1)}, bf16[1,196,1024]{2,1,0:T(8,128)(2,1)}, u32[]{:S(2)}) copy-start(bf16[1,196,1024]{2,1,0:T(8,128)(2,1)} %param.11) | copy-start | bytes 1204228
  7.2 81.9 %all-gather.3.cloned.1.call-start = ((), (), s32[]{:S(2)}) async-start(), calls=%async_computation.3 | async-start | bytes 2621440 | tf_op jit(solution)/shard_map/all_gather | solution.py:21
  11.3 38.1 %copy-start.4 = (f32[1,768]{1,0:T(1,128)S(1)}, f32[1,768]{1,0:T(1,128)}, u32[]{:S(2)}) copy-start(f32[1,768]{1,0:T(1,128)} %param.9) | copy-start | bytes 9220
  91.8 1.2 copy-start.5
  149.1 40.8 %copy-start.1 = (bf16[1,196,1024]{2,1,0:T(8,128)(2,1)S(1)}, bf16[1,196,1024]{2,1,0:T(8,128)(2,1)}, u32[]{:S(2)}) copy-start(bf16[1,196,1024]{2,1,0:T(8,128)(2,1)} %param.6) | copy-start | bytes 1204228
  190.2 1.8 copy-start.2
Sparse Core Ops, SparseCore 0:
  49.5 39.5 all-gather.2
where the time goes:
time: 200 us
  blocking collectives  122 us (61%)
  waiting for transfers between devices  39.7 us (20%)
  matrix products  16.2 us (8%)
  between operations  14.2 us (7%)
  local copies, waits for them, and re-layouts  3.9 us (2%)
  other arithmetic  3.7 us (2%)
    all_to_all x1, blocking collectives, sum_at_owner(): parts = lax.all_to_all(split_up(x, dim, devices), axis, 0, 0, tiled=True)  45 us
    all_to_all x1, blocking collectives, inbound(): lax.all_to_all(summed.astype(jnp.bfloat16), 'expert', split_axis=1, conca...  40 us
    all_gather x1, waiting for transfers between devices, outbound(): return lax.all_gather(moved, 'hidden', axis=1, tiled=True)  39.7 us
    all_to_all x1, blocking collectives, outbound(): lax.all_to_all(stacked, 'expert', split_axis=2, concat_axis=1, tiled=True)  37.1 us
    dot_general x1, matrix products, expert_backward(): jnp.einsum('ref,edf->red', pre_grad, w_in, preferred_element_type=jnp.flo...  6.06 us
  transfers between devices with their start and end apart: 1, of which 1 were waited for; matrix products, arithmetic and copies ran while one was open for 0% of the time, Pallas kernels for 0%

commit v1 on v0

v1 whole, which is shorter than its diff:
```python
import jax
import jax.numpy as jnp
from jax import lax
from jax.sharding import Mesh, PartitionSpec as P

CHIPS = ("expert", "yh")
SPLIT = False


def swap_cores(x):
    return lax.ppermute(x, "core", [(0, 1), (1, 0)])


def exchange(x):
    return lax.all_to_all(x, CHIPS, 0, 0, tiled=True)


def experts(rows, grads, halves):
    value = 0.0
    gvalue = 0.0
    for w_in, b_in, w_out in halves:
        pre = jnp.einsum("rd,df->rf", rows, w_in, preferred_element_type=jnp.float32) + b_in
        act, pull = jax.vjp(jax.nn.gelu, pre)
        value = value + jnp.einsum(
            "rf,fd->rd", act.astype(jnp.bfloat16), w_out, preferred_element_type=jnp.float32
        )
        act_grad = jnp.einsum("rd,fd->rf", grads, w_out, preferred_element_type=jnp.float32)
        pre_grad = pull(act_grad)[0].astype(jnp.bfloat16)
        gvalue = gvalue + jnp.einsum(
            "rf,df->rd", pre_grad, w_in, preferred_element_type=jnp.float32
        )
    return value.astype(jnp.bfloat16), gvalue.astype(jnp.bfloat16)


def shards(tokens, router, w_in, b_in, w_out, cotangent):
    tokens, w_in, w_out, cotangent = tokens[0], w_in[0], w_out[0], cotangent[0]
    own = (w_in, b_in, w_out)
    other = tuple(swap_cores(w) for w in own)
    logits = jnp.einsum("md,ds->ms", tokens, router, preferred_element_type=jnp.float32)
    dispatch = jax.nn.softmax(logits, axis=0)
    combine = jax.nn.softmax(logits, axis=1)
    dispatch_w = dispatch.astype(jnp.bfloat16)
    combine_w = combine.astype(jnp.bfloat16)
    slot_in = jnp.einsum(
        "ms,md->sd", dispatch_w, tokens, preferred_element_type=jnp.float32
    ).astype(jnp.bfloat16)
    slot_cot = jnp.einsum(
        "ms,md->sd", combine_w, cotangent, preferred_element_type=jnp.float32
    ).astype(jnp.bfloat16)
    slots, width = slot_in.shape
    ways = lax.axis_size("yh")
    both = jnp.stack([slot_in, slot_cot], axis=1)
    both = jnp.broadcast_to(both[:, None], (slots, ways, 2, width)).reshape(slots * ways, 2, width)
    arrived = exchange(both)
    value, gvalue = experts(arrived[:, 0], arrived[:, 1], (own, other))
    returned = exchange(jnp.stack([value, gvalue], axis=1)).astype(jnp.float32)
    summed = returned.reshape(slots, ways, 2, width).sum(axis=1).astype(jnp.bfloat16)
    slot_out = summed[:, 0]
    slot_grad = summed[:, 1]
    mixed = jnp.einsum(
        "ms,sd->md", combine_w, slot_out, preferred_element_type=jnp.float32
    ).astype(jnp.bfloat16)
    combine_grad = jnp.einsum(
        "md,sd->ms", cotangent, slot_out, preferred_element_type=jnp.float32
    )
    dispatch_grad = jnp.einsum(
        "md,sd->ms", tokens, slot_grad, preferred_element_type=jnp.float32
    )
    logit_grad = combine * (combine_grad - jnp.sum(combine * combine_grad, axis=1, keepdims=True))
    logit_grad = logit_grad + dispatch * (
        dispatch_grad - jnp.sum(dispatch * dispatch_grad, axis=0, keepdims=True)
    )
    logit_grad = logit_grad.astype(jnp.bfloat16)
    token_grad = jnp.einsum(
        "ms,sd->md", dispatch_w, slot_grad, preferred_element_type=jnp.float32
    )
    token_grad = token_grad + jnp.einsum(
        "ms,ds->md", logit_grad, router, preferred_element_type=jnp.float32
    )
    return mixed[None], token_grad.astype(jnp.bfloat16)[None]


def solution(mesh):
    ways = mesh.shape["hidden"] // 2
    split = Mesh(
        mesh.devices.reshape(mesh.shape["expert"], ways, 2), ("expert", "yh", "core")
    )
    images = P(("expert", "yh", "core"), None, None)
    hidden = ("yh", "core")
    return jax.shard_map(
        shards,
        mesh=split,
        in_specs=(
            images,
            P(),
            P("expert", None, hidden),
            P("expert", hidden),
            P("expert", hidden, None),
            images,
        ),
        out_specs=(images, images),
        check_vma=False,
    )
```

time: 200 us -> 126 us (0.63)
  the two profiles are of different devices: /device:TPU:1 before, /device:TPU:9 now
where the time goes in v1:
time: 126 us; the launch traced here: 124 us
  blocking collectives  39.7 us (32%)
  starting transfers between devices  28.4 us (23%)
  waiting for transfers between devices  25.2 us (20%)
  matrix products  21.3 us (17%)
  local copies, waits for them, and re-layouts  6.61 us (5%)
  other arithmetic  1.89 us (2%)
    all_to_all x1, blocking collectives, exchange(): return lax.all_to_all(x, CHIPS, 0, 0, tiled=True)  39.7 us
    all_to_all x1, waiting for transfers between devices, exchange(): return lax.all_to_all(x, CHIPS, 0, 0, tiled=True)  25.2 us
    all_to_all x1, starting transfers between devices, exchange(): return lax.all_to_all(x, CHIPS, 0, 0, tiled=True)  20.8 us
    dot_general x2, matrix products, experts(): jnp.einsum('rf,df->rd', pre_grad, w_in, preferred_element_type=jnp.float32)  8.39 us
    ppermute x3, starting transfers between devices, swap_cores(): return lax.ppermute(x, 'core', [(0, 1), (1, 0)])  7.66 us
    dot_general x2, matrix products, experts(): jnp.einsum('rf,fd->rd', act.astype(jnp.bfloat16), w_out, preferred_elemen...  4.24 us
    dot_general x2, matrix products, experts(): jnp.einsum('rd,df->rf', rows, w_in, preferred_element_type=jnp.float32)  3.65 us
  transfers between devices with their start and end apart: 4, of which 1 were waited for; matrix products, arithmetic and copies ran while one was open for 9% of the time, Pallas kernels for 0%

profile of v1, /device:TPU:9, one launch (start us, length us, event | category | flops | bytes accessed | tf_op | source)
XLA Modules:
  0.0 124.0 jit_solution(9178989845223827523)
XLA Ops:
  0.6 0.0 copy-start
  0.6 0.0 copy-start.2
  0.7 1.0 copy-done
  1.6 1.3 %fusion.99 = (f32[128]{0:T(128)S(1)}, f32[196]{0:T(256)S(1)}, f32[196,128]{1,0:T(8,128)S(1)}) fusion(bf16[1024,128]{1,0:T(8,128)(2,1)} %param.7, bf16[1,196,1024]{2,1,0:T(8,128)(2,1)S(1)} %copy-done), kind=kOutput, calls=%fused_computation.116 | convolution fusion | flops 51430076 | bytes 765200 | tf_op jit(solution)/shard_map/md,ds->ms/dot_general | solution.py:39
  2.9 0.2 fusion.61
  3.1 0.0 copy-start.3
  3.2 0.3 fusion.7
  3.4 0.2 copy-done.3
  3.7 0.0 copy-done.2
  3.7 0.4 fusion.8
  4.0 0.1 pad_maximum_fusion.1
  4.1 0.5 copy.13
  4.6 0.0 copy-start.5
  4.7 1.5 %broadcast_in_dim.6 = bf16[128,2,2,1024]{3,2,1,0:T(2,128)(2,1)} broadcast(bf16[128,2,1024]{2,1,0:T(2,128)(2,1)S(1)} %copy.13), dimensions={0,2,3} | broadcast | bytes 1572864 | tf_op jit(solution)/shard_map/broadcast_in_dim | solution.py:53
  6.2 20.8 %all-to-all-start = ((bf16[256,2,1024]{2,1,0:T(2,128)(2,1)}), bf16[256,2,1024]{2,1,0:T(2,128)(2,1)S(1)}, u32[]{:S(2)}, u32[]{:S(2)}) async-start(bf16[256,2,1024]{2,1,0:T(2,128)(2,1)} %bitcast.4), calls=%async_computation | async-start | bytes 2097152 | tf_op jit(solution)/shard_map/all_to_all | solution.py:15
  27.0 3.1 %collective-permute-start = (bf16[1024,768]{1,0:T(8,128)(2,1)}, bf16[1024,768]{1,0:T(8,128)(2,1)}, u32[]{:S(2)}, u32[]{:S(2)}) collective-permute-start(bf16[1024,768]{1,0:T(8,128)(2,1)} %bitcast.80), channel_id=1, source_target_pairs={{0,1},{1,0},{2,3},{3,2},{4,5},{5,4},{6,7},{7,6},{8,9},{9,8},{10,11... | collective-permute-start | bytes 4718600 | tf_op jit(solution)/shard_map/ppermute | solution.py:11
  30.1 0.0 copy-done.5
  30.1 1.9 %collective-permute-start.1 = (f32[1,768]{1,0:T(1,128)S(1)}, f32[1,768]{1,0:T(1,128)S(1)}, u32[]{:S(2)}, u32[]{:S(2)}) collective-permute-start(f32[1,768]{1,0:T(1,128)S(1)} %copy-done.5), channel_id=1, source_target_pairs={{0,1},{1,0},{2,3},{3,2},{4,5},{5,4},{6,7},{7,6},{8,9},{9,8},{10,11... | collective-permute-start | bytes 9224 | tf_op jit(solution)/shard_map/ppermute | solution.py:11
  32.0 2.6 %collective-permute-start.2 = (bf16[768,1024]{1,0:T(8,128)(2,1)}, bf16[768,1024]{1,0:T(8,128)(2,1)}, u32[]{:S(2)}, u32[]{:S(2)}) collective-permute-start(bf16[768,1024]{1,0:T(8,128)(2,1)} %bitcast.81), channel_id=1, source_target_pairs={{0,1},{1,0},{2,3},{3,2},{4,5},{5,4},{6,7},{7,6},{8,9},{9,8},{10,11... | collective-permute-start | bytes 4718600 | tf_op jit(solution)/shard_map/ppermute | solution.py:11
  34.7 0.0 collective-permute-done.1
  34.7 25.2 %all-to-all-done = bf16[256,2,1024]{2,1,0:T(2,128)(2,1)S(1)} async-done(((bf16[256,2,1024]{2,1,0:T(2,128)(2,1)}), bf16[256,2,1024]{2,1,0:T(2,128)(2,1)S(1)}, u32[]{:S(2)}, u32[]{:S(2)}) %all-to-all-start) | async-done | bytes 1048608 | tf_op jit(solution)/shard_map/all_to_all | solution.py:15
  59.9 0.0 copy-start.6
  59.9 1.5 %fusion.100 = (bf16[256,1,1024]{2,1,0:T(2,128)(2,1)S(1)}, bf16[256,1,1024]{2,1,0:T(2,128)(2,1)S(1)}) fusion(bf16[256,2,1024]{2,1,0:T(2,128)(2,1)S(1)} %all-to-all-done), kind=kLoop, calls=%fused_computation.117 | loop fusion | bytes 2097152 | tf_op jit(solution)/shard_map/slice | solution.py:55
  61.3 0.0 copy-done.6
  61.4 0.6 convolution_add_fusion.4
  62.0 0.0 copy-start.7
  62.0 0.0 collective-permute-done
  62.0 3.0 %convolution_add_fusion.3 = f32[256,768]{1,0:T(8,128)} fusion(bf16[1024,768]{1,0:T(8,128)(2,1)} %collective-permute-done, f32[768]{0:T(1024)S(1)} %reduce.2, bf16[256,1,1024]{2,1,0:T(2,128)(2,1)S(1)} %get-tuple-element.9), kind=kOutput, calls=%fused_computation.5 | convolution fusion | flops 402849792 | bytes 2886656 | tf_op jit(solution)/shard_map/rd,df->rf/dot_general | solution.py:22
  65.0 0.0 copy-done.7
  65.0 1.6 %fusion.29 = f32[256,1024]{1,0:T(8,128)} fusion(f32[256,768]{1,0:T(8,128)S(1)} %convolution_add_fusion.4, bf16[1,768,1024]{2,1,0:T(8,128)(2,1)S(1)} %copy-done.7), kind=kOutput, calls=%fused_computation.50 | convolution fusion | flops 404422656 | bytes 3407872 | tf_op jit(solution)/shard_map/rf,fd->rd/dot_general | solution.py:24
  66.7 4.4 %fusion.45 = f32[256,1024]{1,0:T(8,128)} fusion(f32[256,768]{1,0:T(8,128)S(1)} %convolution_add_fusion.4, bf16[256,1,1024]{2,1,0:T(2,128)(2,1)S(1)} %get-tuple-element.8, bf16[1,768,1024]{2,1,0:T(8,128)(2,1)} %param.10, bf16[1,1024,768]{2,1,0:T(8,128)(2,1)} %param.8), kind=kOutput, calls=%fused_computation.65 | convolution fusion | flops 809238528 | bytes 5505024 | tf_op jit(solution)/shard_map/rf,df->rd/dot_general | solution.py:29
  71.1 0.0 collective-permute-done.2
  71.1 4.0 %fusion.3 = bf16[256,1,1024]{2,0,1:T(8,128)(2,1)S(1)} fusion(f32[256,1024]{1,0:T(8,128)} %fusion.45, bf16[1024,768]{1,0:T(8,128)(2,1)} %collective-permute-done, f32[256,768]{1,0:T(8,128)} %convolution_add_fusion.3, bf16[768,1024]{1,0:T(8,128)(2,1)} %collective-permute-done.2, bf16[256,1,1024]{2,1,0:T(2,128)(2,1)S(1)} %get-tuple-element.8), kind=kOutput, calls=%fused_computation.9 | convolution fusion | flops 809762816 | bytes 6029312 | tf_op jit(solution)/shard_map/rf,df->rd/dot_general | solution.py:29
  75.1 2.6 %fusion.4 = bf16[256,1,1024]{2,0,1:T(8,128)(2,1)S(1)} fusion(f32[256,1024]{1,0:T(8,128)} %fusion.29, bf16[768,1024]{1,0:T(8,128)(2,1)} %collective-permute-done.2, f32[256,768]{1,0:T(8,128)} %convolution_add_fusion.3), kind=kOutput, calls=%fused_computation.10 | convolution fusion | flops 404946944 | bytes 3932160 | tf_op jit(solution)/shard_map/rf,fd->rd/dot_general | solution.py:24
  77.7 0.1 pad_maximum_fusion
  77.8 1.1 copy.16
  78.9 39.7 %all_to_all.10 = bf16[256,2,1024]{2,1,0:T(2,128)(2,1)S(1)} all-to-all(bf16[256,2,1024]{2,1,0:T(2,128)(2,1)S(1)} %copy.16), channel_id=1, replica_groups=mesh['expert'=128,'yh'=2,'core'=2] {'expert','yh'}, dimensions={0} | all-to-all | bytes 2097152 | tf_op jit(solution)/shard_map/all_to_all | solution.py:15
  118.6 0.0 copy-start.4
  118.6 1.5 %bitcast_reduce_fusion = bf16[128,2,1024]{2,1,0:T(2,128)(2,1)S(1)} fusion(bf16[256,2,1024]{2,1,0:T(2,128)(2,1)S(1)} %all_to_all.10), kind=kLoop, calls=%fused_computation.24 | loop fusion | flops 262144 | bytes 1572864 | tf_op jit(solution)/shard_map/reduce_sum | solution.py:57
  120.1 0.7 fusion.101
  120.8 0.0 copy-done.4
  120.9 0.3 fusion.48
  121.1 0.0 copy-start.1
  121.2 0.3 convolution_bitcast_fusion
  121.4 1.1 fusion.6
  122.5 0.4 multiply_reduce_fusion.1
  122.9 0.0 copy-done.1
  122.9 1.1 fusion.5
  (2 shorter events, 0.0 us)
Async XLA Ops:
  0.6 1.0 copy-start
  0.6 3.0 %copy-start.2 = (bf16[1,196,1024]{2,1,0:T(8,128)(2,1)S(1)}, bf16[1,196,1024]{2,1,0:T(8,128)(2,1)}, u32[]{:S(2)}) copy-start(bf16[1,196,1024]{2,1,0:T(8,128)(2,1)} %param.11) | copy-start | bytes 1204228
  3.1 0.5 copy-start.3
  4.6 25.5 %copy-start.5 = (f32[1,768]{1,0:T(1,128)S(1)}, f32[1,768]{1,0:T(1,128)}, u32[]{:S(2)}) copy-start(f32[1,768]{1,0:T(1,128)} %param.9) | copy-start | bytes 9220
  6.2 53.7 %all-to-all-start = ((bf16[256,2,1024]{2,1,0:T(2,128)(2,1)}), bf16[256,2,1024]{2,1,0:T(2,128)(2,1)S(1)}, u32[]{:S(2)}, u32[]{:S(2)}) async-start(bf16[256,2,1024]{2,1,0:T(2,128)(2,1)} %bitcast.4), calls=%async_computation | async-start | bytes 2097152 | tf_op jit(solution)/shard_map/all_to_all | solution.py:15
  27.0 35.0 %collective-permute-start = (bf16[1024,768]{1,0:T(8,128)(2,1)}, bf16[1024,768]{1,0:T(8,128)(2,1)}, u32[]{:S(2)}, u32[]{:S(2)}) collective-permute-start(bf16[1024,768]{1,0:T(8,128)(2,1)} %bitcast.80), channel_id=1, source_target_pairs={{0,1},{1,0},{2,3},{3,2},{4,5},{5,4},{6,7},{7,6},{8,9},{9,8},{10,11... | collective-permute-start | bytes 4718600 | tf_op jit(solution)/shard_map/ppermute | solution.py:11
  30.1 4.6 %collective-permute-start.1 = (f32[1,768]{1,0:T(1,128)S(1)}, f32[1,768]{1,0:T(1,128)S(1)}, u32[]{:S(2)}, u32[]{:S(2)}) collective-permute-start(f32[1,768]{1,0:T(1,128)S(1)} %copy-done.5), channel_id=1, source_target_pairs={{0,1},{1,0},{2,3},{3,2},{4,5},{5,4},{6,7},{7,6},{8,9},{9,8},{10,11... | collective-permute-start | bytes 9224 | tf_op jit(solution)/shard_map/ppermute | solution.py:11
  32.0 39.1 %collective-permute-start.2 = (bf16[768,1024]{1,0:T(8,128)(2,1)}, bf16[768,1024]{1,0:T(8,128)(2,1)}, u32[]{:S(2)}, u32[]{:S(2)}) collective-permute-start(bf16[768,1024]{1,0:T(8,128)(2,1)} %bitcast.81), channel_id=1, source_target_pairs={{0,1},{1,0},{2,3},{3,2},{4,5},{5,4},{6,7},{7,6},{8,9},{9,8},{10,11... | collective-permute-start | bytes 4718600 | tf_op jit(solution)/shard_map/ppermute | solution.py:11
  59.9 1.5 %copy-start.6 = (bf16[1,1024,768]{2,1,0:T(8,128)(2,1)S(1)}, bf16[1,1024,768]{2,1,0:T(8,128)(2,1)}, u32[]{:S(2)}) copy-start(bf16[1,1024,768]{2,1,0:T(8,128)(2,1)} %param.8) | copy-start | bytes 4718596
  62.0 3.1 %copy-start.7 = (bf16[1,768,1024]{2,1,0:T(8,128)(2,1)S(1)}, bf16[1,768,1024]{2,1,0:T(8,128)(2,1)}, u32[]{:S(2)}) copy-start(bf16[1,768,1024]{2,1,0:T(8,128)(2,1)} %param.10) | copy-start | bytes 4718596
  118.6 2.3 %copy-start.4 = (f32[128]{0:T(128)S(1)}, f32[128]{0:T(128)}, u32[]{:S(2)}) copy-start(f32[128]{0:T(128)} %copy-done.3) | copy-start | bytes 1540
  121.1 1.8 %copy-start.1 = (bf16[1024,128]{1,0:T(8,128)(2,1)S(1)}, bf16[1024,128]{1,0:T(8,128)(2,1)}, u32[]{:S(2)}) copy-start(bf16[1024,128]{1,0:T(8,128)(2,1)} %param.7) | copy-start | bytes 786436

commit v2 on v1

v2 whole, which is shorter than its diff:
```python
import jax
import jax.numpy as jnp
from jax import lax
from jax.experimental import pallas as pl
from jax.experimental.pallas import tpu as pltpu
from jax.sharding import Mesh, PartitionSpec as P

CHIPS = ("expert", "yh")
LANES = 128
UNITS = 256
BLOCKS = 4
PIECES = 1
NN = (((1,), (0,)), ((), ()))
NT = (((1,), (1,)), ((), ()))
TN = (((0,), (0,)), ((), ()))
GELU_A = 0.7978845608028654
GELU_B = 0.044715


def in_hbm(*arrays):
    return [pltpu.with_memory_space_constraint(x, pltpu.HBM) for x in arrays]


def dot(a, b, dims):
    return lax.dot_general(a, b, dims, preferred_element_type=jnp.float32)


def spread(scratch, values, first, step, column):
    rows = values.shape[0]
    for k in range(values.shape[1] // LANES):
        piece = values[:, k * LANES : (k + 1) * LANES]
        scratch[pl.ds(first + column // LANES + k, rows, stride=step), :] = piece


def gather(scratch, out, rows, first, step):
    for k in range(out.shape[1] // LANES):
        piece = scratch[pl.ds(first + k, rows, stride=step), :]
        out[:, k * LANES : (k + 1) * LANES] = piece.astype(out.dtype)


def route_kernel(
    tokens, router, cotangent, sent, dispatch, combine, image, weights, pull, scratch, packed, sems
):
    width = image.shape[2]
    slots = weights.shape[1]
    tiles = 2 * width // LANES
    ways = sent.shape[1] // tiles
    loads = [
        pltpu.make_async_copy(src, dst, sems.at[k])
        for k, (src, dst) in enumerate(((tokens, image), (router, weights), (cotangent, pull)))
    ]
    for load in loads:
        load.start()
    loads[0].wait()
    loads[1].wait()
    logits = dot(image[0], weights[...], NN)
    up = jnp.exp(logits - jnp.max(logits, axis=0, keepdims=True))
    down = up / jnp.sum(up, axis=0, keepdims=True)
    dispatch[...] = down
    down = down.astype(jnp.bfloat16)
    up = jnp.exp(logits - jnp.max(logits, axis=1, keepdims=True))
    across = up / jnp.sum(up, axis=1, keepdims=True)
    combine[...] = across
    across = across.astype(jnp.bfloat16)
    for n in range(0, width, 256):
        spread(scratch, dot(down, image[0, :, n : n + 256], TN), 0, tiles, n)
    loads[2].wait()
    for n in range(0, width, 256):
        spread(scratch, dot(across, pull[0, :, n : n + 256], TN), tiles // 2, tiles, n)
    stores = []
    block = slots // BLOCKS
    for k in range(BLOCKS):
        part = pl.ds(k * block, block)
        piece = scratch[pl.ds(k * block * tiles, block * tiles), :].astype(jnp.bfloat16)
        piece = piece.reshape(block, tiles, LANES)
        for way in range(ways):
            packed[part, way * tiles : (way + 1) * tiles, :] = piece
        stores.append(pltpu.make_async_copy(packed.at[part], sent.at[part], sems.at[3 + k]))
        stores[-1].start()
    for store in stores:
        store.wait()


def route(tokens, router, cotangent, ways):
    _, count, width = tokens.shape
    slots = router.shape[1]
    tiles = 2 * width // LANES
    weights = jax.ShapeDtypeStruct((count, slots), jnp.float32)
    return pl.pallas_call(
        route_kernel,
        out_shape=(
            pltpu.HBM((slots, ways * tiles, LANES), jnp.bfloat16),
            weights,
            weights,
        ),
        in_specs=[pl.BlockSpec(memory_space=pltpu.HBM)] * 3,
        out_specs=(
            pl.BlockSpec(memory_space=pltpu.HBM),
            pl.BlockSpec(memory_space=pltpu.VMEM),
            pl.BlockSpec(memory_space=pltpu.VMEM),
        ),
        scratch_shapes=[
            pltpu.VMEM(tokens.shape, jnp.bfloat16),
            pltpu.VMEM(router.shape, jnp.bfloat16),
            pltpu.VMEM(tokens.shape, jnp.bfloat16),
            pltpu.VMEM((slots * tiles, LANES), jnp.float32),
            pltpu.VMEM((slots, ways * tiles, LANES), jnp.bfloat16),
            pltpu.SemaphoreType.DMA((3 + BLOCKS,)),
        ],
        compiler_params=pltpu.CompilerParams(vmem_limit_bytes=16 * 2**20),
        name="route",
    )(*in_hbm(tokens, router, cotangent))


def expert_kernel(
    arrived, in0, b0, out0, in1, b1, out1, sent, near, first, far, scratch, rows, grads, act, slope, sems
):
    count, tiles, _ = arrived.shape
    half = tiles // 2
    width = half * LANES
    units = b0.shape[1]
    loads = []
    for k, (src, dst) in enumerate(((out0, near), (in1, first), (out1, far))):
        block = dst.shape[0] // PIECES
        loads.append([])
        for p in range(PIECES):
            part = pl.ds(p * block, block)
            copy = pltpu.make_async_copy(src.at[0, part], dst.at[part], sems.at[k, p])
            loads[k].append(copy)
            copy.start()
    scratch[...] = arrived[...].astype(jnp.float32).reshape(count * tiles, LANES)
    gather(scratch, rows, count, 0, tiles)
    gather(scratch, grads, count, half, tiles)
    for h, (w_in, bias, w_out) in enumerate(((in0.at[0], b0, near), (first, b1, far))):
        if h:
            for load in loads[1]:
                load.wait()
        for u in range(0, units, UNITS):
            part = slice(u, u + UNITS)
            at = slice(h * units + u, h * units + u + UNITS)
            pre = dot(rows[...], w_in[:, part], NN) + bias[:, part]
            if u == 0:
                for load in loads[2 * h]:
                    load.wait()
            up = dot(grads[...], w_out[part, :], NT)
            square = pre * pre
            tanh = jnp.tanh(GELU_A * (pre + GELU_B * (square * pre)))
            cdf = 0.5 + 0.5 * tanh
            bend = 0.5 * GELU_A * pre * (1.0 - tanh * tanh) * (1.0 + 3.0 * GELU_B * square)
            act[:, at] = (pre * cdf).astype(jnp.bfloat16)
            slope[:, at] = (up * (cdf + bend)).astype(jnp.bfloat16)
    for n in range(0, width, 256):
        part = slice(n, n + 256)
        value = dot(act[:, :units], near[:, part], NN) + dot(act[:, units:], far[:, part], NN)
        spread(scratch, value, 0, tiles, n)
        value = dot(slope[:, :units], in0[0, part, :], NT) + dot(slope[:, units:], first[part, :], NT)
        spread(scratch, value, half, tiles, n)
    sent[...] = scratch[...].astype(jnp.bfloat16).reshape(count, tiles, LANES)


def experts(arrived, own, other):
    count, tiles, _ = arrived.shape
    width = tiles // 2 * LANES
    units = own[1].shape[1]
    out0, in1, out1 = in_hbm(own[2], other[0], other[2])
    weight = pl.BlockSpec(memory_space=pltpu.HBM)
    local = pl.BlockSpec(memory_space=pltpu.VMEM)
    return pl.pallas_call(
        expert_kernel,
        out_shape=jax.ShapeDtypeStruct(arrived.shape, jnp.bfloat16),
        in_specs=[local, local, local, weight, weight, local, weight],
        out_specs=local,
        scratch_shapes=[
            pltpu.VMEM((units, width), jnp.bfloat16),
            pltpu.VMEM((width, units), jnp.bfloat16),
            pltpu.VMEM((units, width), jnp.bfloat16),
            pltpu.VMEM((count * tiles, LANES), jnp.float32),
            pltpu.VMEM((count, width), jnp.bfloat16),
            pltpu.VMEM((count, width), jnp.bfloat16),
            pltpu.VMEM((count, 2 * units), jnp.bfloat16),
            pltpu.VMEM((count, 2 * units), jnp.bfloat16),
            pltpu.SemaphoreType.DMA((3, PIECES)),
        ],
        compiler_params=pltpu.CompilerParams(vmem_limit_bytes=28 * 2**20),
        name="experts",
    )(arrived, own[0], own[1], out0, in1, other[1], out1)


def finish_kernel(
    returned,
    tokens,
    router,
    cotangent,
    dispatch,
    combine,
    mixed,
    token_grad,
    scratch,
    value,
    grad,
    near,
    far,
    sems,
):
    slots, width = value.shape
    tiles = 2 * width // LANES
    total = returned[:, :tiles, :].astype(jnp.float32)
    for way in range(1, returned.shape[1] // tiles):
        total = total + returned[:, way * tiles : (way + 1) * tiles, :].astype(jnp.float32)
    scratch[...] = total.reshape(slots * tiles, LANES)
    gather(scratch, value, slots, 0, tiles)
    gather(scratch, grad, slots, tiles // 2, tiles)
    down = dispatch[...]
    across = combine[...]
    near[0] = dot(across.astype(jnp.bfloat16), value[...], NN).astype(jnp.bfloat16)
    stores = [pltpu.make_async_copy(near, mixed, sems.at[0])]
    stores[0].start()
    pull = dot(cotangent[0], value[...], NT)
    slope = across * (pull - jnp.sum(across * pull, axis=1, keepdims=True))
    pull = dot(tokens[0], grad[...], NT)
    slope = slope + down * (pull - jnp.sum(down * pull, axis=0, keepdims=True))
    slope = slope.astype(jnp.bfloat16)
    down = down.astype(jnp.bfloat16)
    block = width // BLOCKS
    for k in range(BLOCKS):
        part = pl.ds(k * block, block)
        total = dot(down, grad[:, part], NN) + dot(slope, router[part, :], NT)
        far[0, :, part] = total.astype(jnp.bfloat16)
        stores.append(
            pltpu.make_async_copy(
                far.at[:, :, part], token_grad.at[:, :, part], sems.at[1 + k]
            )
        )
        stores[-1].start()
    for store in stores:
        store.wait()


def finish(returned, tokens, router, cotangent, dispatch, combine):
    width, slots = router.shape
    result = jax.ShapeDtypeStruct(tokens.shape, jnp.bfloat16)
    far = pl.BlockSpec(memory_space=pltpu.HBM)
    local = pl.BlockSpec(memory_space=pltpu.VMEM)
    return pl.pallas_call(
        finish_kernel,
        out_shape=(result, result),
        in_specs=[local] * 6,
        out_specs=(far, far),
        scratch_shapes=[
            pltpu.VMEM((slots * 2 * width // LANES, LANES), jnp.float32),
            pltpu.VMEM((slots, width), jnp.bfloat16),
            pltpu.VMEM((slots, width), jnp.bfloat16),
            pltpu.VMEM(tokens.shape, jnp.bfloat16),
            pltpu.VMEM(tokens.shape, jnp.bfloat16),
            pltpu.SemaphoreType.DMA((1 + BLOCKS,)),
        ],
        compiler_params=pltpu.CompilerParams(vmem_limit_bytes=16 * 2**20),
        name="finish",
    )(returned, tokens, router, cotangent, dispatch, combine)


def swap_cores(x):
    return lax.ppermute(x, "core", [(0, 1), (1, 0)])


def exchange(x):
    return lax.all_to_all(x, CHIPS, 0, 0, tiled=True)


def shards(tokens, router, w_in, b_in, w_out, cotangent):
    slots = router.shape[1]
    ways = lax.axis_size("yh")
    own = (w_in, b_in, w_out)
    other = tuple(swap_cores(w) for w in own)
    sent, dispatch, combine = route(tokens, router, cotangent, ways)
    tiles = sent.shape[1] // ways
    arrived = exchange(sent.reshape(slots * ways, tiles, LANES))
    returned = exchange(experts(arrived, own, other))
    returned = returned.reshape(slots, ways * tiles, LANES)
    return finish(returned, tokens, router, cotangent, dispatch, combine)


def solution(mesh):
    ways = mesh.shape["hidden"] // 2
    split = Mesh(
        mesh.devices.reshape(mesh.shape["expert"], ways, 2), ("expert", "yh", "core")
    )
    images = P(("expert", "yh", "core"), None, None)
    hidden = ("yh", "core")
    return jax.shard_map(
        shards,
        mesh=split,
        in_specs=(
            images,
            P(),
            P("expert", None, hidden),
            P("expert", hidden),
            P("expert", hidden, None),
            images,
        ),
        out_specs=(images, images),
        check_vma=False,
    )
```

time: 126 us -> 108 us (0.86)
  matrix products: 21.3 us -> 0 us
  Pallas kernels: 0 us -> 11.1 us
  local copies, waits for them, and re-layouts: 6.61 us -> 1.18 us
  other arithmetic: 1.89 us -> 0 us
    dot_general x14 -> x0, matrix products: 21.3 us -> none  [the longest x2 8.39 us: experts(): jnp.einsum('rf,df->rd', pre_grad, w_in, preferred_element_type=jnp.float32)]
    pallas_call x0 -> x3, Pallas kernels: none -> 11.1 us  [the longest x1 5.95 us: experts(): pl.pallas_call(expert_kernel, out_shape=jax.ShapeDtypeStruct(arrived.shap...]
    all_to_all x1, waiting for transfers between devices: 25.2 us -> 22.9 us  [exchange(): return lax.all_to_all(x, CHIPS, 0, 0, tiled=True)]
    slice x2 -> x0, local copies, waits for them, and re-layouts: 2.21 us -> none  [the longest x1 1.48 us: shards(): value, gvalue = experts(arrived[:, 0], arrived[:, 1], (own, other))]
    reduce_sum x2 -> x0, other arithmetic: 1.71 us -> none  [the longest x1 1.51 us: shards(): returned.reshape(slots, ways, 2, width).sum(axis=1).astype(jnp.bfloat16)]
    another operation x2 -> x0, local copies, waits for them, and re-layouts: 1.62 us -> none  [the longest x1 1.08 us: shards(): returned = exchange(jnp.stack([value, gvalue], axis=1)).astype(jnp.float32)]
    broadcast_in_dim x1 -> x0, local copies, waits for them, and re-layouts: 1.52 us -> none  [shards(): jnp.broadcast_to(both[:, None], (slots, ways, 2, width))]
    ppermute x3, waiting for transfers between devices: 0.01 us -> 1.3 us  [swap_cores(): return lax.ppermute(x, 'core', [(0, 1), (1, 0)])]
  transfers between devices with their start and end apart: 4 -> 4, of which waited for: 1 -> 2; matrix products, arithmetic and copies ran while one was open for 9% -> 0% of each run, Pallas kernels for 0% -> 0%
where the time goes in v2:
time: 108 us; the launch traced here: 105 us
  blocking collectives  39.8 us (37%)
  starting transfers between devices  28.3 us (26%)
  waiting for transfers between devices  24.2 us (22%)
  Pallas kernels  11.1 us (10%)
  local copies, waits for them, and re-layouts  1.18 us (1%)
    all_to_all x1, blocking collectives, exchange(): return lax.all_to_all(x, CHIPS, 0, 0, tiled=True)  39.8 us
    all_to_all x1, waiting for transfers between devices, exchange(): return lax.all_to_all(x, CHIPS, 0, 0, tiled=True)  22.9 us
    all_to_all x1, starting transfers between devices, exchange(): return lax.all_to_all(x, CHIPS, 0, 0, tiled=True)  20.8 us
    ppermute x3, starting transfers between devices, swap_cores(): return lax.ppermute(x, 'core', [(0, 1), (1, 0)])  7.47 us
    pallas_call x1, Pallas kernels, experts(): pl.pallas_call(expert_kernel, out_shape=jax.ShapeDtypeStruct(arrived.shap...  5.95 us
    pallas_call x1, Pallas kernels, route(): pl.pallas_call(route_kernel, out_shape=(pltpu.HBM((slots, ways * tiles, L...  3.22 us
  transfers between devices with their start and end apart: 4, of which 2 were waited for; matrix products, arithmetic and copies ran while one was open for 0% of the time, Pallas kernels for 0%

profile of v2, /device:TPU:9, one launch (start us, length us, event | category | flops | bytes accessed | tf_op | source)
XLA Modules:
  0.0 105.5 jit_solution(17111834881746271986)
XLA Ops:
  0.6 0.0 copy-start.2
  0.6 0.0 copy-start.4
  0.6 3.2 %route.1 = (bf16[128,32,128]{2,1,0:T(8,128)(2,1)}, f32[196,128]{1,0:T(8,128)S(1)}, f32[196,128]{1,0:T(8,128)S(1)}) custom-call(bf16[1,196,1024]{2,1,0:T(8,128)(2,1)} %tokens.3, bf16[1024,128]{1,0:T(8,128)(2,1)} %router.3, bf16[1,196,1024]{2,1,0:T(8,128)(2,1)} %cotangent.3), custom_call_target="tpu_custom_call" | custom-call | tf_op jit(solution)/shard_map/route/pallas_call | solution.py:89
  3.9 20.8 %all-to-all-start = ((bf16[256,16,128]{2,1,0:T(8,128)(2,1)}), bf16[256,16,128]{2,1,0:T(8,128)(2,1)S(1)}, u32[]{:S(2)}, u32[]{:S(2)}) async-start(bf16[256,16,128]{2,1,0:T(8,128)(2,1)} %bitcast.3), calls=%async_computation | async-start | bytes 2097152 | tf_op jit(solution)/shard_map/all_to_all | solution.py:267
  24.7 0.0 copy-done.2
  24.7 3.1 %collective-permute-start = (bf16[1,1024,768]{2,1,0:T(8,128)(2,1)S(1)}, bf16[1,1024,768]{2,1,0:T(8,128)(2,1)S(1)}, u32[]{:S(2)}, u32[]{:S(2)}) collective-permute-start(bf16[1,1024,768]{2,1,0:T(8,128)(2,1)S(1)} %copy-done.2), channel_id=1, source_target_pairs={{0,1},{1,0},{2,3},{3,2},{4,5},{5,4},{6,7},{7,6},{8,9},{9,8},{10,11... | collective-permute-start | bytes 4718600 | tf_op jit(solution)/shard_map/ppermute | solution.py:263
  27.8 1.9 %collective-permute-start.2 = (bf16[1,768,1024]{2,1,0:T(8,128)(2,1)}, bf16[1,768,1024]{2,1,0:T(8,128)(2,1)}, u32[]{:S(2)}, u32[]{:S(2)}) collective-permute-start(bf16[1,768,1024]{2,1,0:T(8,128)(2,1)} %out0.1), channel_id=1, source_target_pairs={{0,1},{1,0},{2,3},{3,2},{4,5},{5,4},{6,7},{7,6},{8,9},{9,8},{10,11... | collective-permute-start | bytes 4718600 | tf_op jit(solution)/shard_map/ppermute | solution.py:263
  29.8 0.0 copy-done.4
  29.8 2.4 %collective-permute-start.1 = (f32[1,768]{1,0:T(1,128)S(1)}, f32[1,768]{1,0:T(1,128)S(1)}, u32[]{:S(2)}, u32[]{:S(2)}) collective-permute-start(f32[1,768]{1,0:T(1,128)S(1)} %copy-done.4), channel_id=1, source_target_pairs={{0,1},{1,0},{2,3},{3,2},{4,5},{5,4},{6,7},{7,6},{8,9},{9,8},{10,11... | collective-permute-start | bytes 9224 | tf_op jit(solution)/shard_map/ppermute | solution.py:263
  32.2 1.3 %collective-permute-done.1.b1 = f32[1,768]{1,0:T(1,128)S(1)} collective-permute-done((f32[1,768]{1,0:T(1,128)S(1)}, f32[1,768]{1,0:T(1,128)S(1)}, u32[]{:S(2)}, u32[]{:S(2)}) %collective-permute-start.1) | collective-permute-done | bytes 3104 | tf_op jit(solution)/shard_map/ppermute | solution.py:263
  33.5 0.0 collective-permute-done.in1
  33.5 0.0 copy-start.5
  33.5 1.2 %copy-done.5 = bf16[1,1024,768]{2,1,0:T(8,128)(2,1)} copy-done((bf16[1,1024,768]{2,1,0:T(8,128)(2,1)}, bf16[1,1024,768]{2,1,0:T(8,128)(2,1)S(1)}, u32[]{:S(2)}) %copy-start.5) | copy-done | bytes 1572888
  34.6 0.0 collective-permute-done.2.out1
  34.6 22.9 %all-to-all-done.arrived = bf16[256,16,128]{2,1,0:T(8,128)(2,1)S(1)} async-done(((bf16[256,16,128]{2,1,0:T(8,128)(2,1)}), bf16[256,16,128]{2,1,0:T(8,128)(2,1)S(1)}, u32[]{:S(2)}, u32[]{:S(2)}) %all-to-all-start) | async-done | bytes 1048608 | tf_op jit(solution)/shard_map/all_to_all | solution.py:267
  57.6 6.0 %experts.1 = bf16[256,16,128]{2,1,0:T(8,128)(2,1)S(1)} custom-call(bf16[256,16,128]{2,1,0:T(8,128)(2,1)S(1)} %all-to-all-done.arrived, bf16[1,1024,768]{2,1,0:T(8,128)(2,1)S(1)} %copy-done.2, f32[1,768]{1,0:T(1,128)S(1)} %copy-done.4, bf16[1,768,1024]{2,1,0:T(8,128)(2,1)} %out0.1, bf16[1,1024,768]{2,1,0:T(8,128)(2,1)} %copy-done.5, ...), custom_call_target="tpu_custom_call" | custom-call | tf_op jit(solution)/shard_map/experts/pallas_call | solution.py:168
  63.5 0.0 copy-start
  63.6 0.0 copy-start.1
  63.6 0.0 copy-start.3
  63.6 39.8 %all_to_all.10 = bf16[256,16,128]{2,1,0:T(8,128)(2,1)S(1)} all-to-all(bf16[256,16,128]{2,1,0:T(8,128)(2,1)S(1)} %experts.1), channel_id=1, replica_groups=mesh['expert'=128,'yh'=2,'core'=2] {'expert','yh'}, dimensions={0} | all-to-all | bytes 2097152 | tf_op jit(solution)/shard_map/all_to_all | solution.py:267
  103.4 0.0 copy-done
  103.4 0.0 copy-done.1
  103.4 0.0 copy-done.3
  103.4 1.9 %finish.1 = (bf16[1,196,1024]{2,1,0:T(8,128)(2,1)}, bf16[1,196,1024]{2,1,0:T(8,128)(2,1)}) custom-call(bf16[128,32,128]{2,1,0:T(8,128)(2,1)S(1)} %bitcast.2, bf16[1,196,1024]{2,1,0:T(8,128)(2,1)S(1)} %copy-done, bf16[1024,128]{1,0:T(8,128)(2,1)S(1)} %copy-done.3, bf16[1,196,1024]{2,1,0:T(8,128)(2,1)S(1)} %copy-done.1, ...), custom_call_target="tpu_custom_call" | custom-call | tf_op jit(solution)/shard_map/finish/pallas_call | solution.py:244
Async XLA Ops:
  0.6 24.0 %copy-start.2 = (bf16[1,1024,768]{2,1,0:T(8,128)(2,1)S(1)}, bf16[1,1024,768]{2,1,0:T(8,128)(2,1)}, u32[]{:S(2)}) copy-start(bf16[1,1024,768]{2,1,0:T(8,128)(2,1)} %in0.1) | copy-start | bytes 4718596
  0.6 29.1 %copy-start.4 = (f32[1,768]{1,0:T(1,128)S(1)}, f32[1,768]{1,0:T(1,128)}, u32[]{:S(2)}) copy-start(f32[1,768]{1,0:T(1,128)} %b0.1) | copy-start | bytes 9220
  3.9 53.7 %all-to-all-start = ((bf16[256,16,128]{2,1,0:T(8,128)(2,1)}), bf16[256,16,128]{2,1,0:T(8,128)(2,1)S(1)}, u32[]{:S(2)}, u32[]{:S(2)}) async-start(bf16[256,16,128]{2,1,0:T(8,128)(2,1)} %bitcast.3), calls=%async_computation | async-start | bytes 2097152 | tf_op jit(solution)/shard_map/all_to_all | solution.py:267
  24.7 8.8 %collective-permute-start = (bf16[1,1024,768]{2,1,0:T(8,128)(2,1)S(1)}, bf16[1,1024,768]{2,1,0:T(8,128)(2,1)S(1)}, u32[]{:S(2)}, u32[]{:S(2)}) collective-permute-start(bf16[1,1024,768]{2,1,0:T(8,128)(2,1)S(1)} %copy-done.2), channel_id=1, source_target_pairs={{0,1},{1,0},{2,3},{3,2},{4,5},{5,4},{6,7},{7,6},{8,9},{9,8},{10,11... | collective-permute-start | bytes 4718600 | tf_op jit(solution)/shard_map/ppermute | solution.py:263
  27.8 6.8 %collective-permute-start.2 = (bf16[1,768,1024]{2,1,0:T(8,128)(2,1)}, bf16[1,768,1024]{2,1,0:T(8,128)(2,1)}, u32[]{:S(2)}, u32[]{:S(2)}) collective-permute-start(bf16[1,768,1024]{2,1,0:T(8,128)(2,1)} %out0.1), channel_id=1, source_target_pairs={{0,1},{1,0},{2,3},{3,2},{4,5},{5,4},{6,7},{7,6},{8,9},{9,8},{10,11... | collective-permute-start | bytes 4718600 | tf_op jit(solution)/shard_map/ppermute | solution.py:263
  29.8 3.7 %collective-permute-start.1 = (f32[1,768]{1,0:T(1,128)S(1)}, f32[1,768]{1,0:T(1,128)S(1)}, u32[]{:S(2)}, u32[]{:S(2)}) collective-permute-start(f32[1,768]{1,0:T(1,128)S(1)} %copy-done.4), channel_id=1, source_target_pairs={{0,1},{1,0},{2,3},{3,2},{4,5},{5,4},{6,7},{7,6},{8,9},{9,8},{10,11... | collective-permute-start | bytes 9224 | tf_op jit(solution)/shard_map/ppermute | solution.py:263
  33.5 1.2 %copy-start.5 = (bf16[1,1024,768]{2,1,0:T(8,128)(2,1)}, bf16[1,1024,768]{2,1,0:T(8,128)(2,1)S(1)}, u32[]{:S(2)}) copy-start(bf16[1,1024,768]{2,1,0:T(8,128)(2,1)S(1)} %collective-permute-done.in1) | copy-start | bytes 4718596
  63.5 39.9 %copy-start = (bf16[1,196,1024]{2,1,0:T(8,128)(2,1)S(1)}, bf16[1,196,1024]{2,1,0:T(8,128)(2,1)}, u32[]{:S(2)}) copy-start(bf16[1,196,1024]{2,1,0:T(8,128)(2,1)} %tokens.3) | copy-start | bytes 1204228
  63.6 39.9 %copy-start.1 = (bf16[1,196,1024]{2,1,0:T(8,128)(2,1)S(1)}, bf16[1,196,1024]{2,1,0:T(8,128)(2,1)}, u32[]{:S(2)}) copy-start(bf16[1,196,1024]{2,1,0:T(8,128)(2,1)} %cotangent.3) | copy-start | bytes 1204228
  63.6 39.9 %copy-start.3 = (bf16[1024,128]{1,0:T(8,128)(2,1)S(1)}, bf16[1024,128]{1,0:T(8,128)(2,1)}, u32[]{:S(2)}) copy-start(bf16[1024,128]{1,0:T(8,128)(2,1)} %router.3) | copy-start | bytes 786436

commit v3 on v2

--- a/solution.py
+++ b/solution.py
@@ -9,7 +9,7 @@
 LANES = 128
 UNITS = 256
 BLOCKS = 4
-PIECES = 1
+STAGGER_NS = 11000
 NN = (((1,), (0,)), ((), ()))
 NT = (((1,), (1,)), ((), ()))
 TN = (((0,), (0,)), ((), ()))
@@ -39,7 +39,7 @@
 
 
 def route_kernel(
-    tokens, router, cotangent, sent, dispatch, combine, image, weights, pull, scratch, packed, sems
+    late, tokens, router, cotangent, sent, dispatch, combine, image, weights, pull, scratch, packed, sems
 ):
     width = image.shape[2]
     slots = weights.shape[1]
@@ -79,9 +79,10 @@
         stores[-1].start()
     for store in stores:
         store.wait()
-
-
-def route(tokens, router, cotangent, ways):
+    pl.delay(late[0])
+
+
+def route(late, tokens, router, cotangent, ways):
     _, count, width = tokens.shape
     slots = router.shape[1]
     tiles = 2 * width // LANES
@@ -93,7 +94,8 @@
             weights,
             weights,
         ),
-        in_specs=[pl.BlockSpec(memory_space=pltpu.HBM)] * 3,
+        in_specs=[pl.BlockSpec(memory_space=pltpu.SMEM)]
+        + [pl.BlockSpec(memory_space=pltpu.HBM)] * 3,
         out_specs=(
             pl.BlockSpec(memory_space=pltpu.HBM),
             pl.BlockSpec(memory_space=pltpu.VMEM),
@@ -109,39 +111,26 @@
         ],
         compiler_params=pltpu.CompilerParams(vmem_limit_bytes=16 * 2**20),
         name="route",
-    )(*in_hbm(tokens, router, cotangent))
+    )(late, *in_hbm(tokens, router, cotangent))
 
 
 def expert_kernel(
-    arrived, in0, b0, out0, in1, b1, out1, sent, near, first, far, scratch, rows, grads, act, slope, sems
+    arrived, in0, b0, out0, in1, b1, out1, sent, scratch, rows, grads, act, slope
 ):
     count, tiles, _ = arrived.shape
     half = tiles // 2
     width = half * LANES
     units = b0.shape[1]
-    loads = []
-    for k, (src, dst) in enumerate(((out0, near), (in1, first), (out1, far))):
-        block = dst.shape[0] // PIECES
-        loads.append([])
-        for p in range(PIECES):
-            part = pl.ds(p * block, block)
-            copy = pltpu.make_async_copy(src.at[0, part], dst.at[part], sems.at[k, p])
-            loads[k].append(copy)
-            copy.start()
     scratch[...] = arrived[...].astype(jnp.float32).reshape(count * tiles, LANES)
     gather(scratch, rows, count, 0, tiles)
     gather(scratch, grads, count, half, tiles)
-    for h, (w_in, bias, w_out) in enumerate(((in0.at[0], b0, near), (first, b1, far))):
-        if h:
-            for load in loads[1]:
-                load.wait()
+    for h, (w_in, bias, w_out) in enumerate(
+        ((in0.at[0], b0, out0.at[0]), (in1.at[0], b1, out1.at[0]))
+    ):
         for u in range(0, units, UNITS):
             part = slice(u, u + UNITS)
             at = slice(h * units + u, h * units + u + UNITS)
             pre = dot(rows[...], w_in[:, part], NN) + bias[:, part]
-            if u == 0:
-                for load in loads[2 * h]:
-                    load.wait()
             up = dot(grads[...], w_out[part, :], NT)
             square = pre * pre
             tanh = jnp.tanh(GELU_A * (pre + GELU_B * (square * pre)))
@@ -151,9 +140,9 @@
             slope[:, at] = (up * (cdf + bend)).astype(jnp.bfloat16)
     for n in range(0, width, 256):
         part = slice(n, n + 256)
-        value = dot(act[:, :units], near[:, part], NN) + dot(act[:, units:], far[:, part], NN)
+        value = dot(act[:, :units], out0[0, :, part], NN) + dot(act[:, units:], out1[0, :, part], NN)
         spread(scratch, value, 0, tiles, n)
-        value = dot(slope[:, :units], in0[0, part, :], NT) + dot(slope[:, units:], first[part, :], NT)
+        value = dot(slope[:, :units], in0[0, part, :], NT) + dot(slope[:, units:], in1[0, part, :], NT)
         spread(scratch, value, half, tiles, n)
     sent[...] = scratch[...].astype(jnp.bfloat16).reshape(count, tiles, LANES)
 
@@ -162,28 +151,22 @@
     count, tiles, _ = arrived.shape
     width = tiles // 2 * LANES
     units = own[1].shape[1]
-    out0, in1, out1 = in_hbm(own[2], other[0], other[2])
-    weight = pl.BlockSpec(memory_space=pltpu.HBM)
     local = pl.BlockSpec(memory_space=pltpu.VMEM)
     return pl.pallas_call(
         expert_kernel,
         out_shape=jax.ShapeDtypeStruct(arrived.shape, jnp.bfloat16),
-        in_specs=[local, local, local, weight, weight, local, weight],
+        in_specs=[local] * 7,
         out_specs=local,
         scratch_shapes=[
-            pltpu.VMEM((units, width), jnp.bfloat16),
-            pltpu.VMEM((width, units), jnp.bfloat16),
-            pltpu.VMEM((units, width), jnp.bfloat16),
             pltpu.VMEM((count * tiles, LANES), jnp.float32),
             pltpu.VMEM((count, width), jnp.bfloat16),
             pltpu.VMEM((count, width), jnp.bfloat16),
             pltpu.VMEM((count, 2 * units), jnp.bfloat16),
             pltpu.VMEM((count, 2 * units), jnp.bfloat16),
-            pltpu.SemaphoreType.DMA((3, PIECES)),
         ],
         compiler_params=pltpu.CompilerParams(vmem_limit_bytes=28 * 2**20),
         name="experts",
-    )(arrived, own[0], own[1], out0, in1, other[1], out1)
+    )(arrived, *own, *other)
 
 
 def finish_kernel(
@@ -272,7 +255,9 @@
     ways = lax.axis_size("yh")
     own = (w_in, b_in, w_out)
     other = tuple(swap_cores(w) for w in own)
-    sent, dispatch, combine = route(tokens, router, cotangent, ways)
+    late = (lax.axis_index("core") * STAGGER_NS).reshape(1)
+    sent, dispatch, combine = route(late, tokens, router, cotangent, ways)
+    sent, *other = lax.optimization_barrier((sent, *other))
     tiles = sent.shape[1] // ways
     arrived = exchange(sent.reshape(slots * ways, tiles, LANES))
     returned = exchange(experts(arrived, own, other))

time: 108 us -> 107 us (level); the launches traced: 105 us -> 107 us
  blocking collectives: 39.8 us -> 78.3 us
  waiting for transfers between devices: 24.2 us -> 0.01 us
  starting transfers between devices: 28.3 us -> 6.91 us
  Pallas kernels: 11.1 us -> 20.8 us
  local copies, waits for them, and re-layouts: 1.18 us -> 0.03 us
    all_to_all x1 -> x2, blocking collectives: 39.8 us -> 78.3 us  [exchange(): return lax.all_to_all(x, CHIPS, 0, 0, tiled=True)]
    all_to_all x1 -> x0, waiting for transfers between devices: 22.9 us -> none  [exchange(): return lax.all_to_all(x, CHIPS, 0, 0, tiled=True)]
    all_to_all x1 -> x0, starting transfers between devices: 20.8 us -> none  [exchange(): return lax.all_to_all(x, CHIPS, 0, 0, tiled=True)]
    pallas_call x1, Pallas kernels: 3.22 us -> 14.2 us  [route(): pl.pallas_call(route_kernel, out_shape=(pltpu.HBM((slots, ways * tiles, L...]
    ppermute x3, waiting for transfers between devices: 1.3 us -> 0.01 us  [swap_cores(): return lax.ppermute(x, 'core', [(0, 1), (1, 0)])]
    pallas_call x1, Pallas kernels: 5.95 us -> 4.71 us  [experts(): pl.pallas_call(expert_kernel, out_shape=jax.ShapeDtypeStruct(arrived.shap...]
    unnamed x12, local copies, waits for them, and re-layouts: 1.18 us -> 0.03 us
  transfers between devices with their start and end apart: 4 -> 3, of which waited for: 2 -> 0; matrix products, arithmetic and copies ran while one was open for 0% -> 0% of each run, Pallas kernels for 0% -> 13%
where the time goes in v3:
time: 107 us
  blocking collectives  78.3 us (73%)
  Pallas kernels  20.8 us (19%)
  starting transfers between devices  6.91 us (6%)
    all_to_all x2, blocking collectives, exchange(): return lax.all_to_all(x, CHIPS, 0, 0, tiled=True)  78.3 us
    pallas_call x1, Pallas kernels, route(): pl.pallas_call(route_kernel, out_shape=(pltpu.HBM((slots, ways * tiles, L...  14.2 us
    ppermute x3, starting transfers between devices, swap_cores(): return lax.ppermute(x, 'core', [(0, 1), (1, 0)])  6.91 us
    pallas_call x1, Pallas kernels, experts(): pl.pallas_call(expert_kernel, out_shape=jax.ShapeDtypeStruct(arrived.shap...  4.71 us
  transfers between devices with their start and end apart: 3, of which 0 were waited for; matrix products, arithmetic and copies ran while one was open for 0% of the time, Pallas kernels for 13%

profile of v3, /device:TPU:9, one launch (start us, length us, event | category | flops | bytes accessed | tf_op | source)
XLA Modules:
  0.0 107.0 jit_solution(7040658123969921795)
XLA Ops:
  0.6 2.6 %collective-permute-start = (bf16[1,1024,768]{2,1,0:T(8,128)(2,1)}, bf16[1,1024,768]{2,1,0:T(8,128)(2,1)S(1)}, u32[]{:S(2)}, u32[]{:S(2)}) collective-permute-start(bf16[1,1024,768]{2,1,0:T(8,128)(2,1)} %in0.1), channel_id=1, source_target_pairs={{0,1},{1,0},{2,3},{3,2},{4,5},{5,4},{6,7},{7,6},{8,9},{9,8},{10,11... | collective-permute-start | bytes 4718600 | tf_op jit(solution)/shard_map/ppermute | solution.py:246
  3.2 1.9 %collective-permute-start.2 = (bf16[1,768,1024]{2,1,0:T(8,128)(2,1)}, bf16[1,768,1024]{2,1,0:T(8,128)(2,1)S(1)}, u32[]{:S(2)}, u32[]{:S(2)}) collective-permute-start(bf16[1,768,1024]{2,1,0:T(8,128)(2,1)} %out0.1), channel_id=1, source_target_pairs={{0,1},{1,0},{2,3},{3,2},{4,5},{5,4},{6,7},{7,6},{8,9},{9,8},{10,11... | collective-permute-start | bytes 4718600 | tf_op jit(solution)/shard_map/ppermute | solution.py:246
  5.1 2.4 %collective-permute-start.1 = (f32[1,768]{1,0:T(1,128)}, f32[1,768]{1,0:T(1,128)S(1)}, u32[]{:S(2)}, u32[]{:S(2)}) collective-permute-start(f32[1,768]{1,0:T(1,128)} %b0.1), channel_id=1, source_target_pairs={{0,1},{1,0},{2,3},{3,2},{4,5},{5,4},{6,7},{7,6},{8,9},{9,8},{10,11... | collective-permute-start | bytes 9224 | tf_op jit(solution)/shard_map/ppermute | solution.py:246
  7.6 0.0 copy-start.2
  7.6 0.0 copy-start.3
  7.6 0.0 copy-start.5
  7.6 14.2 %route.1 = (bf16[128,32,128]{2,1,0:T(8,128)(2,1)}, f32[196,128]{1,0:T(8,128)S(1)}, f32[196,128]{1,0:T(8,128)S(1)}) custom-call(s32[1]{0:T(128)} %bitcast.late, bf16[1,196,1024]{2,1,0:T(8,128)(2,1)} %tokens.3, bf16[1024,128]{1,0:T(8,128)(2,1)} %router.3, bf16[1,196,1024]{2,1,0:T(8,128)(2,1)} %cotangent.3), custom_call_target="tpu_custom_call" | custom-call | tf_op jit(solution)/shard_map/route/pallas_call | solution.py:90
  21.8 0.0 collective-permute-done.1.b1
  21.8 0.0 collective-permute-done.in1
  21.8 0.0 collective-permute-done.2.out1
  21.9 44.6 %all_to_all.10.arrived = bf16[256,16,128]{2,1,0:T(8,128)(2,1)S(1)} all-to-all(bf16[256,16,128]{2,1,0:T(8,128)(2,1)} %bitcast.4), channel_id=1, replica_groups=mesh['expert'=128,'yh'=2,'core'=2] {'expert','yh'}, dimensions={0} | all-to-all | bytes 2097152 | tf_op jit(solution)/shard_map/all_to_all | solution.py:250
  66.5 0.0 copy-done.2
  66.5 0.0 copy-done.3
  66.5 0.0 copy-done.5
  66.5 4.7 %experts.1 = bf16[256,16,128]{2,1,0:T(8,128)(2,1)S(1)} custom-call(bf16[256,16,128]{2,1,0:T(8,128)(2,1)S(1)} %all_to_all.10.arrived, bf16[1,1024,768]{2,1,0:T(8,128)(2,1)S(1)} %copy-done.2, f32[1,768]{1,0:T(1,128)S(1)} %copy-done.5, bf16[1,768,1024]{2,1,0:T(8,128)(2,1)S(1)} %copy-done.3, bf16[1,1024,768]{2,1,0:T(8,128)(2,1)S(1)} %collective-permute-done.in1, ...), custom_call_target="tpu_custom_call" | custom-call | tf_op jit(solution)/shard_map/experts/pallas_call | solution.py:155
  71.2 0.0 copy-start
  71.2 0.0 copy-start.1
  71.2 0.0 copy-start.4
  71.2 33.7 %all_to_all.11 = bf16[256,16,128]{2,1,0:T(8,128)(2,1)S(1)} all-to-all(bf16[256,16,128]{2,1,0:T(8,128)(2,1)S(1)} %experts.1), channel_id=1, replica_groups=mesh['expert'=128,'yh'=2,'core'=2] {'expert','yh'}, dimensions={0} | all-to-all | bytes 2097152 | tf_op jit(solution)/shard_map/all_to_all | solution.py:250
  104.9 0.0 copy-done
  104.9 0.0 copy-done.1
  104.9 0.0 copy-done.4
  104.9 1.9 %finish.1 = (bf16[1,196,1024]{2,1,0:T(8,128)(2,1)}, bf16[1,196,1024]{2,1,0:T(8,128)(2,1)}) custom-call(bf16[128,32,128]{2,1,0:T(8,128)(2,1)S(1)} %bitcast.3, bf16[1,196,1024]{2,1,0:T(8,128)(2,1)S(1)} %copy-done, bf16[1024,128]{1,0:T(8,128)(2,1)S(1)} %copy-done.4, bf16[1,196,1024]{2,1,0:T(8,128)(2,1)S(1)} %copy-done.1, ...), custom_call_target="tpu_custom_call" | custom-call | tf_op jit(solution)/shard_map/finish/pallas_call | solution.py:227
Async XLA Ops:
  0.6 21.2 %collective-permute-start = (bf16[1,1024,768]{2,1,0:T(8,128)(2,1)}, bf16[1,1024,768]{2,1,0:T(8,128)(2,1)S(1)}, u32[]{:S(2)}, u32[]{:S(2)}) collective-permute-start(bf16[1,1024,768]{2,1,0:T(8,128)(2,1)} %in0.1), channel_id=1, source_target_pairs={{0,1},{1,0},{2,3},{3,2},{4,5},{5,4},{6,7},{7,6},{8,9},{9,8},{10,11... | collective-permute-start | bytes 4718600 | tf_op jit(solution)/shard_map/ppermute | solution.py:246
  3.2 18.6 %collective-permute-start.2 = (bf16[1,768,1024]{2,1,0:T(8,128)(2,1)}, bf16[1,768,1024]{2,1,0:T(8,128)(2,1)S(1)}, u32[]{:S(2)}, u32[]{:S(2)}) collective-permute-start(bf16[1,768,1024]{2,1,0:T(8,128)(2,1)} %out0.1), channel_id=1, source_target_pairs={{0,1},{1,0},{2,3},{3,2},{4,5},{5,4},{6,7},{7,6},{8,9},{9,8},{10,11... | collective-permute-start | bytes 4718600 | tf_op jit(solution)/shard_map/ppermute | solution.py:246
  5.1 16.7 %collective-permute-start.1 = (f32[1,768]{1,0:T(1,128)}, f32[1,768]{1,0:T(1,128)S(1)}, u32[]{:S(2)}, u32[]{:S(2)}) collective-permute-start(f32[1,768]{1,0:T(1,128)} %b0.1), channel_id=1, source_target_pairs={{0,1},{1,0},{2,3},{3,2},{4,5},{5,4},{6,7},{7,6},{8,9},{9,8},{10,11... | collective-permute-start | bytes 9224 | tf_op jit(solution)/shard_map/ppermute | solution.py:246
  7.6 58.9 %copy-start.2 = (bf16[1,1024,768]{2,1,0:T(8,128)(2,1)S(1)}, bf16[1,1024,768]{2,1,0:T(8,128)(2,1)}, u32[]{:S(2)}) copy-start(bf16[1,1024,768]{2,1,0:T(8,128)(2,1)} %in0.1) | copy-start | bytes 4718596
  7.6 58.9 %copy-start.3 = (bf16[1,768,1024]{2,1,0:T(8,128)(2,1)S(1)}, bf16[1,768,1024]{2,1,0:T(8,128)(2,1)}, u32[]{:S(2)}) copy-start(bf16[1,768,1024]{2,1,0:T(8,128)(2,1)} %out0.1) | copy-start | bytes 4718596
  7.6 58.9 %copy-start.5 = (f32[1,768]{1,0:T(1,128)S(1)}, f32[1,768]{1,0:T(1,128)}, u32[]{:S(2)}) copy-start(f32[1,768]{1,0:T(1,128)} %b0.1) | copy-start | bytes 9220
  71.2 33.7 %copy-start = (bf16[1,196,1024]{2,1,0:T(8,128)(2,1)S(1)}, bf16[1,196,1024]{2,1,0:T(8,128)(2,1)}, u32[]{:S(2)}) copy-start(bf16[1,196,1024]{2,1,0:T(8,128)(2,1)} %tokens.3) | copy-start | bytes 1204228
  71.2 33.7 %copy-start.1 = (bf16[1,196,1024]{2,1,0:T(8,128)(2,1)S(1)}, bf16[1,196,1024]{2,1,0:T(8,128)(2,1)}, u32[]{:S(2)}) copy-start(bf16[1,196,1024]{2,1,0:T(8,128)(2,1)} %cotangent.3) | copy-start | bytes 1204228
  71.2 33.7 %copy-start.4 = (bf16[1024,128]{1,0:T(8,128)(2,1)S(1)}, bf16[1024,128]{1,0:T(8,128)(2,1)}, u32[]{:S(2)}) copy-start(bf16[1024,128]{1,0:T(8,128)(2,1)} %router.3) | copy-start | bytes 786436

commit v4 on v2

--- a/solution.py
+++ b/solution.py
@@ -10,6 +10,7 @@
 UNITS = 256
 BLOCKS = 4
 PIECES = 1
+STAGGER_NS = 8000
 NN = (((1,), (0,)), ((), ()))
 NT = (((1,), (1,)), ((), ()))
 TN = (((0,), (0,)), ((), ()))
@@ -39,7 +40,7 @@
 
 
 def route_kernel(
-    tokens, router, cotangent, sent, dispatch, combine, image, weights, pull, scratch, packed, sems
+    late, tokens, router, cotangent, sent, dispatch, combine, image, weights, pull, scratch, packed, sems
 ):
     width = image.shape[2]
     slots = weights.shape[1]
@@ -79,9 +80,10 @@
         stores[-1].start()
     for store in stores:
         store.wait()
-
-
-def route(tokens, router, cotangent, ways):
+    pl.delay(late[0])
+
+
+def route(late, tokens, router, cotangent, ways):
     _, count, width = tokens.shape
     slots = router.shape[1]
     tiles = 2 * width // LANES
@@ -93,7 +95,8 @@
             weights,
             weights,
         ),
-        in_specs=[pl.BlockSpec(memory_space=pltpu.HBM)] * 3,
+        in_specs=[pl.BlockSpec(memory_space=pltpu.SMEM)]
+        + [pl.BlockSpec(memory_space=pltpu.HBM)] * 3,
         out_specs=(
             pl.BlockSpec(memory_space=pltpu.HBM),
             pl.BlockSpec(memory_space=pltpu.VMEM),
@@ -109,7 +112,7 @@
         ],
         compiler_params=pltpu.CompilerParams(vmem_limit_bytes=16 * 2**20),
         name="route",
-    )(*in_hbm(tokens, router, cotangent))
+    )(late, *in_hbm(tokens, router, cotangent))
 
 
 def expert_kernel(
@@ -272,7 +275,8 @@
     ways = lax.axis_size("yh")
     own = (w_in, b_in, w_out)
     other = tuple(swap_cores(w) for w in own)
-    sent, dispatch, combine = route(tokens, router, cotangent, ways)
+    late = (lax.axis_index("core") * STAGGER_NS).reshape(1)
+    sent, dispatch, combine = route(late, tokens, router, cotangent, ways)
     tiles = sent.shape[1] // ways
     arrived = exchange(sent.reshape(slots * ways, tiles, LANES))
     returned = exchange(experts(arrived, own, other))

time: 108 us -> 107 us (level); the launches traced: 105 us -> 106 us
  Pallas kernels: 11.1 us -> 19.1 us
  waiting for transfers between devices: 24.2 us -> 20 us
  blocking collectives: 39.8 us -> 38.2 us
  starting transfers between devices: 28.3 us -> 27 us
    pallas_call x1, Pallas kernels: 3.22 us -> 11.2 us  [route(): pl.pallas_call(route_kernel, out_shape=(pltpu.HBM((slots, ways * tiles, L...]
    all_to_all x1, waiting for transfers between devices: 22.9 us -> 18.6 us  [exchange(): return lax.all_to_all(x, CHIPS, 0, 0, tiled=True)]
    all_to_all x1, blocking collectives: 39.8 us -> 38.2 us  [exchange(): return lax.all_to_all(x, CHIPS, 0, 0, tiled=True)]
    ppermute x3, starting transfers between devices: 7.47 us -> 6.25 us  [swap_cores(): return lax.ppermute(x, 'core', [(0, 1), (1, 0)])]
where the time goes in v4:
time: 107 us; the launch traced here: 106 us
  blocking collectives  38.2 us (36%)
  starting transfers between devices  27 us (25%)
  waiting for transfers between devices  20 us (19%)
  Pallas kernels  19.1 us (18%)
  local copies, waits for them, and re-layouts  1.18 us (1%)
    all_to_all x1, blocking collectives, exchange(): return lax.all_to_all(x, CHIPS, 0, 0, tiled=True)  38.2 us
    all_to_all x1, starting transfers between devices, exchange(): return lax.all_to_all(x, CHIPS, 0, 0, tiled=True)  20.8 us
    all_to_all x1, waiting for transfers between devices, exchange(): return lax.all_to_all(x, CHIPS, 0, 0, tiled=True)  18.6 us
    pallas_call x1, Pallas kernels, route(): pl.pallas_call(route_kernel, out_shape=(pltpu.HBM((slots, ways * tiles, L...  11.2 us
    ppermute x3, starting transfers between devices, swap_cores(): return lax.ppermute(x, 'core', [(0, 1), (1, 0)])  6.25 us
    pallas_call x1, Pallas kernels, experts(): pl.pallas_call(expert_kernel, out_shape=jax.ShapeDtypeStruct(arrived.shap...  5.96 us
  transfers between devices with their start and end apart: 4, of which 2 were waited for; matrix products, arithmetic and copies ran while one was open for 0% of the time, Pallas kernels for 0%

profile of v4, /device:TPU:9, one launch (start us, length us, event | category | flops | bytes accessed | tf_op | source)
XLA Modules:
  0.0 106.4 jit_solution(8912890143412111105)
XLA Ops:
  0.6 0.0 copy-start.2
  0.6 0.0 copy-start.4
  0.7 11.2 %route.1 = (bf16[128,32,128]{2,1,0:T(8,128)(2,1)}, f32[196,128]{1,0:T(8,128)S(1)}, f32[196,128]{1,0:T(8,128)S(1)}) custom-call(s32[1]{0:T(128)} %bitcast.late, bf16[1,196,1024]{2,1,0:T(8,128)(2,1)} %tokens.3, bf16[1024,128]{1,0:T(8,128)(2,1)} %router.3, bf16[1,196,1024]{2,1,0:T(8,128)(2,1)} %cotangent.3), custom_call_target="tpu_custom_call" | custom-call | tf_op jit(solution)/shard_map/route/pallas_call | solution.py:91
  11.9 20.8 %all-to-all-start = ((bf16[256,16,128]{2,1,0:T(8,128)(2,1)}), bf16[256,16,128]{2,1,0:T(8,128)(2,1)S(1)}, u32[]{:S(2)}, u32[]{:S(2)}) async-start(bf16[256,16,128]{2,1,0:T(8,128)(2,1)} %bitcast.4), calls=%async_computation | async-start | bytes 2097152 | tf_op jit(solution)/shard_map/all_to_all | solution.py:270
  32.7 0.0 copy-done.2
  32.7 1.9 %collective-permute-start = (bf16[1,1024,768]{2,1,0:T(8,128)(2,1)S(1)}, bf16[1,1024,768]{2,1,0:T(8,128)(2,1)S(1)}, u32[]{:S(2)}, u32[]{:S(2)}) collective-permute-start(bf16[1,1024,768]{2,1,0:T(8,128)(2,1)S(1)} %copy-done.2), channel_id=1, source_target_pairs={{0,1},{1,0},{2,3},{3,2},{4,5},{5,4},{6,7},{7,6},{8,9},{9,8},{10,11... | collective-permute-start | bytes 4718600 | tf_op jit(solution)/shard_map/ppermute | solution.py:266
  34.6 2.4 %collective-permute-start.2 = (bf16[1,768,1024]{2,1,0:T(8,128)(2,1)}, bf16[1,768,1024]{2,1,0:T(8,128)(2,1)}, u32[]{:S(2)}, u32[]{:S(2)}) collective-permute-start(bf16[1,768,1024]{2,1,0:T(8,128)(2,1)} %out0.1), channel_id=1, source_target_pairs={{0,1},{1,0},{2,3},{3,2},{4,5},{5,4},{6,7},{7,6},{8,9},{9,8},{10,11... | collective-permute-start | bytes 4718600 | tf_op jit(solution)/shard_map/ppermute | solution.py:266
  37.0 0.0 copy-done.4
  37.0 1.9 %collective-permute-start.1 = (f32[1,768]{1,0:T(1,128)S(1)}, f32[1,768]{1,0:T(1,128)S(1)}, u32[]{:S(2)}, u32[]{:S(2)}) collective-permute-start(f32[1,768]{1,0:T(1,128)S(1)} %copy-done.4), channel_id=1, source_target_pairs={{0,1},{1,0},{2,3},{3,2},{4,5},{5,4},{6,7},{7,6},{8,9},{9,8},{10,11... | collective-permute-start | bytes 9224 | tf_op jit(solution)/shard_map/ppermute | solution.py:266
  39.0 1.4 %collective-permute-done.1.b1 = f32[1,768]{1,0:T(1,128)S(1)} collective-permute-done((f32[1,768]{1,0:T(1,128)S(1)}, f32[1,768]{1,0:T(1,128)S(1)}, u32[]{:S(2)}, u32[]{:S(2)}) %collective-permute-start.1) | collective-permute-done | bytes 3104 | tf_op jit(solution)/shard_map/ppermute | solution.py:266
  40.4 0.0 collective-permute-done.in1
  40.4 0.0 copy-start.5
  40.4 1.2 %copy-done.5 = bf16[1,1024,768]{2,1,0:T(8,128)(2,1)} copy-done((bf16[1,1024,768]{2,1,0:T(8,128)(2,1)}, bf16[1,1024,768]{2,1,0:T(8,128)(2,1)S(1)}, u32[]{:S(2)}) %copy-start.5) | copy-done | bytes 1572888
  41.5 0.0 collective-permute-done.2.out1
  41.5 18.6 %all-to-all-done.arrived = bf16[256,16,128]{2,1,0:T(8,128)(2,1)S(1)} async-done(((bf16[256,16,128]{2,1,0:T(8,128)(2,1)}), bf16[256,16,128]{2,1,0:T(8,128)(2,1)S(1)}, u32[]{:S(2)}, u32[]{:S(2)}) %all-to-all-start) | async-done | bytes 1048608 | tf_op jit(solution)/shard_map/all_to_all | solution.py:270
  60.2 6.0 %experts.1 = bf16[256,16,128]{2,1,0:T(8,128)(2,1)S(1)} custom-call(bf16[256,16,128]{2,1,0:T(8,128)(2,1)S(1)} %all-to-all-done.arrived, bf16[1,1024,768]{2,1,0:T(8,128)(2,1)S(1)} %copy-done.2, f32[1,768]{1,0:T(1,128)S(1)} %copy-done.4, bf16[1,768,1024]{2,1,0:T(8,128)(2,1)} %out0.1, bf16[1,1024,768]{2,1,0:T(8,128)(2,1)} %copy-done.5, ...), custom_call_target="tpu_custom_call" | custom-call | tf_op jit(solution)/shard_map/experts/pallas_call | solution.py:171
  66.1 0.0 copy-start
  66.1 0.0 copy-start.1
  66.2 0.0 copy-start.3
  66.2 38.2 %all_to_all.10 = bf16[256,16,128]{2,1,0:T(8,128)(2,1)S(1)} all-to-all(bf16[256,16,128]{2,1,0:T(8,128)(2,1)S(1)} %experts.1), channel_id=1, replica_groups=mesh['expert'=128,'yh'=2,'core'=2] {'expert','yh'}, dimensions={0} | all-to-all | bytes 2097152 | tf_op jit(solution)/shard_map/all_to_all | solution.py:270
  104.4 0.0 copy-done
  104.4 0.0 copy-done.1
  104.4 0.0 copy-done.3
  104.4 1.9 %finish.1 = (bf16[1,196,1024]{2,1,0:T(8,128)(2,1)}, bf16[1,196,1024]{2,1,0:T(8,128)(2,1)}) custom-call(bf16[128,32,128]{2,1,0:T(8,128)(2,1)S(1)} %bitcast.3, bf16[1,196,1024]{2,1,0:T(8,128)(2,1)S(1)} %copy-done, bf16[1024,128]{1,0:T(8,128)(2,1)S(1)} %copy-done.3, bf16[1,196,1024]{2,1,0:T(8,128)(2,1)S(1)} %copy-done.1, ...), custom_call_target="tpu_custom_call" | custom-call | tf_op jit(solution)/shard_map/finish/pallas_call | solution.py:247
Async XLA Ops:
  0.6 32.0 %copy-start.2 = (bf16[1,1024,768]{2,1,0:T(8,128)(2,1)S(1)}, bf16[1,1024,768]{2,1,0:T(8,128)(2,1)}, u32[]{:S(2)}) copy-start(bf16[1,1024,768]{2,1,0:T(8,128)(2,1)} %in0.1) | copy-start | bytes 4718596
  0.6 36.4 %copy-start.4 = (f32[1,768]{1,0:T(1,128)S(1)}, f32[1,768]{1,0:T(1,128)}, u32[]{:S(2)}) copy-start(f32[1,768]{1,0:T(1,128)} %b0.1) | copy-start | bytes 9220
  11.9 48.3 %all-to-all-start = ((bf16[256,16,128]{2,1,0:T(8,128)(2,1)}), bf16[256,16,128]{2,1,0:T(8,128)(2,1)S(1)}, u32[]{:S(2)}, u32[]{:S(2)}) async-start(bf16[256,16,128]{2,1,0:T(8,128)(2,1)} %bitcast.4), calls=%async_computation | async-start | bytes 2097152 | tf_op jit(solution)/shard_map/all_to_all | solution.py:270
  32.7 7.7 %collective-permute-start = (bf16[1,1024,768]{2,1,0:T(8,128)(2,1)S(1)}, bf16[1,1024,768]{2,1,0:T(8,128)(2,1)S(1)}, u32[]{:S(2)}, u32[]{:S(2)}) collective-permute-start(bf16[1,1024,768]{2,1,0:T(8,128)(2,1)S(1)} %copy-done.2), channel_id=1, source_target_pairs={{0,1},{1,0},{2,3},{3,2},{4,5},{5,4},{6,7},{7,6},{8,9},{9,8},{10,11... | collective-permute-start | bytes 4718600 | tf_op jit(solution)/shard_map/ppermute | solution.py:266
  34.6 6.9 %collective-permute-start.2 = (bf16[1,768,1024]{2,1,0:T(8,128)(2,1)}, bf16[1,768,1024]{2,1,0:T(8,128)(2,1)}, u32[]{:S(2)}, u32[]{:S(2)}) collective-permute-start(bf16[1,768,1024]{2,1,0:T(8,128)(2,1)} %out0.1), channel_id=1, source_target_pairs={{0,1},{1,0},{2,3},{3,2},{4,5},{5,4},{6,7},{7,6},{8,9},{9,8},{10,11... | collective-permute-start | bytes 4718600 | tf_op jit(solution)/shard_map/ppermute | solution.py:266
  37.0 3.3 %collective-permute-start.1 = (f32[1,768]{1,0:T(1,128)S(1)}, f32[1,768]{1,0:T(1,128)S(1)}, u32[]{:S(2)}, u32[]{:S(2)}) collective-permute-start(f32[1,768]{1,0:T(1,128)S(1)} %copy-done.4), channel_id=1, source_target_pairs={{0,1},{1,0},{2,3},{3,2},{4,5},{5,4},{6,7},{7,6},{8,9},{9,8},{10,11... | collective-permute-start | bytes 9224 | tf_op jit(solution)/shard_map/ppermute | solution.py:266
  40.4 1.2 %copy-start.5 = (bf16[1,1024,768]{2,1,0:T(8,128)(2,1)}, bf16[1,1024,768]{2,1,0:T(8,128)(2,1)S(1)}, u32[]{:S(2)}) copy-start(bf16[1,1024,768]{2,1,0:T(8,128)(2,1)S(1)} %collective-permute-done.in1) | copy-start | bytes 4718596
  66.1 38.2 %copy-start = (bf16[1,196,1024]{2,1,0:T(8,128)(2,1)S(1)}, bf16[1,196,1024]{2,1,0:T(8,128)(2,1)}, u32[]{:S(2)}) copy-start(bf16[1,196,1024]{2,1,0:T(8,128)(2,1)} %tokens.3) | copy-start | bytes 1204228
  66.1 38.2 %copy-start.1 = (bf16[1,196,1024]{2,1,0:T(8,128)(2,1)S(1)}, bf16[1,196,1024]{2,1,0:T(8,128)(2,1)}, u32[]{:S(2)}) copy-start(bf16[1,196,1024]{2,1,0:T(8,128)(2,1)} %cotangent.3) | copy-start | bytes 1204228
  66.2 38.2 %copy-start.3 = (bf16[1024,128]{1,0:T(8,128)(2,1)S(1)}, bf16[1024,128]{1,0:T(8,128)(2,1)}, u32[]{:S(2)}) copy-start(bf16[1024,128]{1,0:T(8,128)(2,1)} %router.3) | copy-start | bytes 786436
